TPU v7x, 32 devices: a whole 2x2x4 slice. The times are simulated.
32 devices in a mesh: context: 2 (over core), tensor: 4 (over y, x), fsdp: 4 (over z).
Axes of the slice: x: 2, y: 2, z: 4, core: 2. Of those that a mesh axis runs over, the one named last changes fastest.
Arguments:
- input_raw: bfloat16 [4, 1024, 5120], P('fsdp', ('context', 'tensor')), may hold values from -6 to 6
- state_proj_raw: bfloat16 [4, 1024, 256], P('fsdp', ('context', 'tensor')), may hold values from -6 to 6
- gate_branch: bfloat16 [4, 1024, 5120], P('fsdp', ('context', 'tensor')), may hold values from -6 to 6
- step_raw: bfloat16 [4, 1024, 80], P('fsdp', ('context', 'tensor')), may hold values from -6 to 6
- convolution_taps: float32 [4, 5376], replicated, may hold values from -3 to 3
- convolution_bias: float32 [5376], replicated, may hold values from -3 to 3
- step_bias: float32 [80], P('tensor'), may hold values from -1.5 to 0.5
- decay_log_rate: float32 [80], P('tensor'), may hold values from -13 to -2, as said below
- skip_weight: float32 [80], P('tensor'), may hold values from 0.5 to 2
- gated_norm_gain: float32 [5120], P('tensor'), may hold values from 0.1 to 1.9
- output_weight: bfloat16 [5120, 2560], P('tensor', 'fsdp'), may hold values from -0.078125 to 0.078125
- adapter_down: bfloat16 [5120, 16], P('tensor'), may hold values from -0.078125 to 0.078125
- adapter_up: bfloat16 [16, 2560], replicated, may hold values from -0.29882812 to 0.29882812
- cotangent: bfloat16 [4, 1024, 2560], P('fsdp', ('context', 'tensor')), may hold values from -6 to 6
Outputs:
- mixed: bfloat16 [4, 1024, 2560], P('fsdp', ('context', 'tensor'))
- grad_a: float32 [5120, 16], P('tensor')
- grad_b: float32 [16, 2560], replicated
Inputs may be any that keep to these rules, and one draw needn't show every extreme that they name: `decay_log_rate`: logarithms of positive decay rates.
All inputs are finite; a program needn't handle non-finite values.
Results may differ from a plain program's by a relative error of at most 0.017.
Values may be sent and summed in bfloat16 or wider, within the bound.
A program may use at most 128 MiB of HBM per device.

v0:
```python
import math

import jax
import jax.numpy as jnp
from jax import lax
from jax.sharding import PartitionSpec as P

epsilon = 1e-05


def passed_along(value, axis, steps):
    count = lax.axis_size(axis)
    leading, last = (max(0, -steps), min(count, count - steps))
    return lax.ppermute(value, axis, [(source, source + steps) for source in range(leading, last)])


def entering(value, axis, join, neutral):
    count, mine = (lax.axis_size(axis), lax.axis_index(axis))
    pieces = jax.tree.map(lambda part: lax.all_gather(part, axis), value)
    subtotal = jax.tree.map(
        lambda part, zero: jnp.full_like(part, 0) + jnp.asarray(zero, part.dtype), value, neutral
    )

    def lap(position, subtotal):
        longer = join(subtotal, jax.tree.map(lambda part: part[position], pieces))
        return jax.tree.map(lambda new, old: jnp.where(position < mine, new, old), longer, subtotal)

    return lax.fori_loop(0, count - 1, lap, subtotal)


def convolve(values, before, weight, bias_row):
    length = values.shape[0]
    extended = jnp.concatenate([before, values], axis=0)
    pre_act = bias_row[None, :] + weight[0][None, :] * extended[0:length].astype(jnp.float32)
    for tap_index in range(1, weight.shape[0]):
        pre_act = pre_act + weight[tap_index][None, :] * extended[
            tap_index : tap_index + length
        ].astype(jnp.float32)
    return jax.nn.silu(pre_act).astype(jnp.bfloat16)


def ssd_blocks(x_heads, b_rows, c_rows, step_size, log_decay, block_len):
    highest = lax.Precision.HIGHEST
    length = x_heads.shape[0]
    head_count = x_heads.shape[1]
    head_size = x_heads.shape[2]
    state_size = b_rows.shape[1]
    blocks = length // block_len
    causal = jnp.arange(block_len)[:, None] >= jnp.arange(block_len)[None, :]

    def advance(state_now, pieces):
        x_block, b_block, c_block, step_block, decay_block = pieces
        cum_decay = jnp.cumsum(decay_block, axis=0)
        cum_heads = cum_decay.T
        gap_decay = cum_heads[:, :, None] - cum_heads[:, None, :]
        decay_mat = jnp.where(causal[None], jnp.exp(jnp.where(causal[None], gap_decay, 0.0)), 0.0)
        gram_mat = jnp.dot(c_block, b_block.T, precision=highest)
        x_scaled = x_block * step_block[:, :, None]
        y_inner = jnp.einsum(
            "hij,jhp->ihp", decay_mat * gram_mat[None], x_scaled, precision=highest
        )
        y_state = jnp.exp(cum_decay)[:, :, None] * jnp.einsum(
            "in,hpn->ihp", c_block, state_now, precision=highest
        )
        tail_decay = jnp.exp(cum_decay[-1][None, :] - cum_decay)
        state_next = jnp.exp(cum_decay[-1])[:, None, None] * state_now + jnp.einsum(
            "jhp,jn->hpn", x_scaled * tail_decay[:, :, None], b_block, precision=highest
        )
        return (state_next, y_inner + y_state)

    start_state = jnp.zeros((head_count, head_size, state_size), jnp.float32)
    state_end, y_blocks = lax.scan(
        advance,
        start_state,
        (
            x_heads.reshape(blocks, block_len, head_count, head_size),
            b_rows.reshape(blocks, block_len, state_size),
            c_rows.reshape(blocks, block_len, state_size),
            step_size.reshape(blocks, block_len, head_count),
            log_decay.reshape(blocks, block_len, head_count),
        ),
    )
    return (y_blocks.reshape(length, head_count, head_size), state_end)


def chain_states(earlier, later):
    return (earlier[0] + later[0], jnp.exp(later[0])[:, None, None] * earlier[1] + later[1])


def row_slice(values, start_row, row_count):
    return lax.dynamic_slice_in_dim(values, start_row, row_count, 0)


def shards(
    input_raw,
    state_proj_raw,
    gate_branch,
    step_raw,
    convolution_taps,
    convolution_bias,
    step_bias,
    decay_log_rate,
    skip_weight,
    gated_norm_gain,
    output_weight,
    adapter_down,
    adapter_up,
    cotangent,
):
    highest = lax.Precision.HIGHEST
    tok_rows = input_raw.shape[1]
    inner_width = input_raw.shape[2]
    state_size = state_proj_raw.shape[2] // 2
    rim_width = convolution_taps.shape[0] - 1
    joined = jnp.concatenate([input_raw[0], state_proj_raw[0]], axis=1)
    before = passed_along(joined[tok_rows - rim_width :], ("context", "tensor"), 1)
    convolved = convolve(joined, before, convolution_taps, convolution_bias)
    x_heads_raw, z_heads, dt_heads = (
        lax.all_to_all(
            convolved[:, :inner_width], "tensor", split_axis=1, concat_axis=0, tiled=True
        ),
        lax.all_to_all(gate_branch[0], "tensor", split_axis=1, concat_axis=0, tiled=True),
        lax.all_to_all(step_raw[0], "tensor", split_axis=1, concat_axis=0, tiled=True),
    )
    shared = lax.all_gather(convolved[:, inner_width:], "tensor", axis=0, tiled=True)
    span_rows = x_heads_raw.shape[0]
    local_heads = dt_heads.shape[1]
    local_width = x_heads_raw.shape[1]
    head_size = local_width // local_heads
    x_heads = x_heads_raw.astype(jnp.float32).reshape(span_rows, local_heads, head_size)
    b_rows = shared[:, :state_size].astype(jnp.float32)
    c_rows = shared[:, state_size:].astype(jnp.float32)
    step_size = jax.nn.softplus(dt_heads.astype(jnp.float32) + step_bias[None, :])
    log_decay = -step_size * jnp.exp(decay_log_rate)[None, :]
    y_local, state_end = ssd_blocks(
        x_heads, b_rows, c_rows, step_size, log_decay, math.gcd(span_rows, 256)
    )
    log_total = jnp.sum(log_decay, axis=0)
    prior_total, incoming = entering(
        (log_total, state_end),
        "context",
        chain_states,
        (jnp.zeros_like(log_total), jnp.zeros_like(state_end)),
    )
    reach_decay = jnp.exp(jnp.cumsum(log_decay, axis=0))
    y_heads = y_local + reach_decay[:, :, None] * jnp.einsum(
        "tn,hpn->thp", c_rows, incoming, precision=highest
    )
    y_heads = y_heads + skip_weight[None, :, None] * x_heads
    gated = y_heads.reshape(span_rows, local_width) * jax.nn.silu(z_heads.astype(jnp.float32))
    squares = jnp.sum(gated * gated, axis=1)
    gated_output = (gated * gated_norm_gain[None, :]).astype(jnp.bfloat16)
    adapter_piece = jnp.dot(gated_output, adapter_down, preferred_element_type=jnp.float32)
    full_width = local_width * lax.axis_size("tensor")
    columns = lax.all_gather(output_weight, "fsdp", axis=1, tiled=True)
    own_start = lax.axis_index("tensor") * tok_rows
    sum_squares, adapter_all = (
        lax.psum(squares.astype(jnp.bfloat16), "tensor").astype(jnp.float32),
        lax.psum(adapter_piece.astype(jnp.bfloat16), "tensor").astype(jnp.float32),
    )
    scale_all = lax.rsqrt(sum_squares / full_width + epsilon)
    adapter_all = adapter_all.astype(jnp.bfloat16)
    leader = (lax.axis_index("tensor") == 0).astype(jnp.float32)
    start_row = jnp.int32(0)
    frozen_piece = jnp.dot(
        row_slice(gated_output, start_row, lax.axis_size("tensor") * tok_rows),
        columns,
        preferred_element_type=jnp.float32,
    )
    frozen_piece = frozen_piece + 2.0 * leader * jnp.dot(
        row_slice(adapter_all, start_row, lax.axis_size("tensor") * tok_rows),
        adapter_up,
        preferred_element_type=jnp.float32,
    )
    summed = lax.psum_scatter(
        (
            row_slice(scale_all, start_row, lax.axis_size("tensor") * tok_rows)[:, None]
            * frozen_piece
        ).astype(jnp.bfloat16),
        "tensor",
        scatter_dimension=0,
        tiled=True,
    )
    row_norm_scale = row_slice(scale_all, own_start, tok_rows)
    adapter_branch = row_slice(adapter_all, own_start, tok_rows)
    cotangent_rows = cotangent[0]
    token_total = (
        tok_rows * lax.axis_size("context") * lax.axis_size("tensor") * lax.axis_size("fsdp")
    )
    lowrank_factor = 2.0 / math.sqrt(token_total)
    weighted = lowrank_factor * row_norm_scale[:, None] * adapter_branch.astype(jnp.float32)
    grad_b_local = jnp.dot(weighted.T, cotangent_rows.astype(jnp.float32), precision=highest)
    adapter_gradient = (
        lowrank_factor
        * row_norm_scale[:, None]
        * jnp.dot(cotangent_rows, adapter_up.T, preferred_element_type=jnp.float32)
    )
    adapter_span = lax.all_gather(adapter_gradient, "tensor", axis=0, tiled=True)
    grad_a_local = jnp.dot(gated_output.astype(jnp.float32).T, adapter_span, precision=highest)
    grad_a, grad_b_part = lax.psum((grad_a_local, grad_b_local), ("context", "fsdp"))
    grad_b = lax.psum(grad_b_part.astype(jnp.bfloat16), "tensor").astype(jnp.float32)
    return (summed[None], grad_a, grad_b)


def solution(mesh):
    placed = (
        P("fsdp", ("context", "tensor"), None),
        P("fsdp", ("context", "tensor"), None),
        P("fsdp", ("context", "tensor"), None),
        P("fsdp", ("context", "tensor"), None),
        P(),
        P(),
        P("tensor"),
        P("tensor"),
        P("tensor"),
        P("tensor"),
        P("tensor", "fsdp"),
        P("tensor", None),
        P(),
        P("fsdp", ("context", "tensor"), None),
    )
    return jax.shard_map(
        shards,
        mesh=mesh,
        in_specs=placed,
        out_specs=(P("fsdp", ("context", "tensor"), None), P("tensor", None), P()),
        check_vma=False,
    )
```

profile of v0, /device:TPU:24, one launch (start us, length us, event | category | flops | bytes accessed | tf_op | source)
XLA Modules:
  0.0 441.6 jit_solution(7496762377417726398)
XLA Ops:
  7.2 1.1 fusion.75
  8.3 3.4 collective-permute-start
  11.7 1.3 all_to_all.30
  13.0 3.3 all-to-all-start
  16.3 1.3 slice_reduce_fusion.6
  17.6 1.7 maximum_maximum_fusion
  19.4 2.1 multiply_convert_fusion.1
  21.6 1.5 copy.81
  23.1 4.2 all-to-all-start.1
  27.3 0.6 copy-done.12
  28.0 0.8 negate_multiply_fusion
  28.8 19.2 %all_gather.21 = bf16[512,256]{1,0:T(8,128)(2,1)S(1)} all-gather(bf16[128,256]{1,0:T(8,128)(2,1)S(1)} %slice.84), channel_id=1, replica_groups=mesh['context'=2,'tensor'=4,'fsdp'=4] {'tensor'}, dimensions={0}, use_global_device_ids=true | all-gather | bytes 327680 | tf_op jit(solution)/shard_map/all_gather | solution.py:125
  48.0 0.7 copy-done.9
  48.7 0.7 convert.15
  49.6 5.4 %copy.68 = f32[4,128,1280]{1,0,2:T(4,128)S(1)} copy(f32[4,128,1280]{1,2,0:T(8,128)S(1)} %convert_bitcast_fusion.1) | data formatting | bytes 5242880 | tf_op jit(solution)/shard_map/convert_element_type | solution.py:130
  55.1 3.4 reshape.159
  58.4 93.5 %while.4 = (s32[]{:T(128)}, f32[20,64,128]{2,1,0:T(8,128)}, f32[2,256,20,64]{1,0,3,2:T(2,128)}, f32[2,256,20]{1,0,2:T(2,128)}, f32[2,256,20,64]{1,0,3,2:T(2,128)...) while((s32[]{:T(128)}, f32[20,64,128]{2,1,0:T(8,128)}, ...), condition=%wide.region_3.4_spmd.clone.clone, body=%wide.region_0.3_spmd.clone.clone.sunk | while | flops 2122191872 | bytes 18280176 | solution.py:72
  58.4 0.8 constant_dynamic-slice_fusion.6
  60.3 1.3 fusion.114
  61.6 3.1 constant_dynamic-slice_fusion.5
  64.7 6.0 %fusion.115 = f32[256,20,64]{0,2,1:T(8,128)S(1)} fusion(f32[256,256]{1,0:T(8,128)S(1)} %fusion.114, f32[20,256]{1,0:T(8,128)S(1)} %bitcast.176, pred[256,256]{1,0:T(8,128)(4,1)S(1)} %iota_compare_fusion.2, f32[1,256,20,64]{1,0,3,2:T(1,128)S(1)} %constant_dynamic-slice_fusion.5, f32[256,20]{0,1:T(8,128)S(1)} %bitcast.180), kind=kOutput, calls=%fused_computation.15.clone.1 | convolution fusion | flops 1012203520 | bytes 2990080 | tf_op jit(solution)/shard_map/while/body/eval_jaxpr/hij,jhp->ihp/dot_general | solution.py:59
  70.9 0.7 bitcast_exponential_fusion.2
  71.6 2.1 fusion.116
  73.7 1.3 copy.124
  75.1 27.0 %dynamic_update_slice.7 = f32[2,256,20,64]{1,0,3,2:T(2,128)} dynamic-update-slice(f32[2,256,20,64]{1,0,3,2:T(2,128)} %get-tuple-element.267, f32[1,256,20,64]{1,0,3,2:T(1,128)S(1)} %copy.124, s32[]{:T(128)} %get-tuple-element.265, s32[]{:T(128)} %constant.41.clone.1..sunk, s32[]{:T(128)} %constant.41.clone.1..sunk, s32[]{:T(128)} %constant.41.clone.1..sunk) | dynamic-update-slice | bytes 2621444 | tf_op jit(solution)/shard_map/while/body/jit(dynamic_update_index_in_dim)/dynamic_update_slice | solution.py:72
  102.1 2.8 fusion.113
  104.9 0.8 constant_dynamic-slice_fusion.6
  105.8 0.6 reduce-window.28
  106.7 1.3 fusion.114
  108.0 3.1 constant_dynamic-slice_fusion.5
  111.2 6.0 %fusion.115 = f32[256,20,64]{0,2,1:T(8,128)S(1)} fusion(f32[256,256]{1,0:T(8,128)S(1)} %fusion.114, f32[20,256]{1,0:T(8,128)S(1)} %bitcast.176, pred[256,256]{1,0:T(8,128)(4,1)S(1)} %iota_compare_fusion.2, f32[1,256,20,64]{1,0,3,2:T(1,128)S(1)} %constant_dynamic-slice_fusion.5, f32[256,20]{0,1:T(8,128)S(1)} %bitcast.180), kind=kOutput, calls=%fused_computation.15.clone.1 | convolution fusion | flops 1012203520 | bytes 2990080 | tf_op jit(solution)/shard_map/while/body/eval_jaxpr/hij,jhp->ihp/dot_general | solution.py:59
  117.3 0.7 bitcast_exponential_fusion.2
  118.0 2.4 fusion.116
  120.4 1.3 copy.124
  121.8 27.0 %dynamic_update_slice.7 = f32[2,256,20,64]{1,0,3,2:T(2,128)} dynamic-update-slice(f32[2,256,20,64]{1,0,3,2:T(2,128)} %get-tuple-element.267, f32[1,256,20,64]{1,0,3,2:T(1,128)S(1)} %copy.124, s32[]{:T(128)} %get-tuple-element.265, s32[]{:T(128)} %constant.41.clone.1..sunk, s32[]{:T(128)} %constant.41.clone.1..sunk, s32[]{:T(128)} %constant.41.clone.1..sunk) | dynamic-update-slice | bytes 2621444 | tf_op jit(solution)/shard_map/while/body/jit(dynamic_update_index_in_dim)/dynamic_update_slice | solution.py:72
  148.8 3.2 fusion.113
  152.1 0.7 all-gather.5.cloned.1.call-update
  153.3 1.5 copy.77
  154.8 3.5 all-to-all-start.2
  159.8 1.4 reduce-window.16
  161.6 0.6 copy.94
  162.7 2.4 all-reduce
  165.1 6.9 %all-to-all-done.2 = bf16[128,4,1280]{0,2,1:T(8,128)(2,1)S(1)} async-done(((bf16[128,4,1280]{0,2,1:T(8,128)(2,1)}), bf16[128,4,1280]{0,2,1:T(8,128)(2,1)S(1)}, u32[]{:S(2)}, u32[]{:S(2)}) %all-to-all-start.2) | async-done | bytes 1310752 | tf_op jit(solution)/shard_map/all_to_all | solution.py:122
  172.0 0.6 copy.78
  172.7 2.0 convert_bitcast_fusion
  174.7 4.3 copy.79
  179.0 4.3 reshape.166
  183.2 2.1 reshape.165
  185.3 4.9 %reshape.152 = f32[512,20,64]{0,2,1:T(8,128)} reshape(f32[2,256,20,64]{1,0,3,2:T(2,128)} %get-tuple-element.72) | data formatting | bytes 5242880 | tf_op jit(solution)/shard_map/reshape | solution.py:83
  190.3 6.3 %multiply_reduce_fusion = (bf16[512]{0:T(512)(128)(2,1)S(1)}, f32[512,20,64]{0,2,1:T(8,128)}) fusion(f32[512,20,64]{0,2,1:T(8,128)S(1)} %copy-done.6, f32[512,20,64]{0,2,1:T(8,128)} %reshape.165, f32[20]{0:T(128)S(1)} %copy-done.22, f32[512,20,64]{0,2,1:T(8,128)} %reshape.152, f32[40,64,128]{2,1,0:T(8,128)} %all-gather.7.cloned.1.call-done, ...), kind=kOutput, calls=%fused_computation.66 | convolution fusion | flops 1014169088 | bytes 11323393 | tf_op jit(solution)/shard_map/tn,hpn->thp/dot_general | solution.py:146
  196.6 3.4 copy.80
  200.0 2.7 fusion.52
  203.1 15.3 %all-reduce.1 = (bf16[512,16]{0,1:T(8,128)(2,1)S(1)}, bf16[512]{0:T(512)(128)(2,1)S(1)}) all-reduce(bf16[512,16]{0,1:T(8,128)(2,1)S(1)} %convolution_convert_fusion, bf16[512]{0:T(512)(128)(2,1)S(1)} %get-tuple-element.195), channel_id=1, replica_groups=mesh['context'=2,'tensor'=4,'fsdp'=4] {'tensor'}, use_global_device_ids=true, to_apply=%region_9.10 | all-reduce | flops 8704 | bytes 34816 | tf_op jit(solution)/shard_map/psum | solution.py:159
  219.1 8.2 %all_gather.27 = f32[512,16]{0,1:T(8,128)S(1)} all-gather(f32[128,16]{0,1:T(8,128)S(1)} %convolution_multiply_fusion.1), channel_id=1, replica_groups=mesh['context'=2,'tensor'=4,'fsdp'=4] {'tensor'}, dimensions={0}, use_global_device_ids=true | all-gather | bytes 40960 | tf_op jit(solution)/shard_map/all_gather | solution.py:198
  227.3 48.1 %all-reduce.9 = bf16[16,2560]{1,0:T(8,128)(2,1)} all-reduce(f32[16,2560]{1,0:T(8,128)S(1)} %fusion.55), channel_id=1, replica_groups=mesh['context'=2,'tensor'=4,'fsdp'=4] {'context','fsdp'}, use_global_device_ids=true, to_apply=%region_12.13 | all-reduce | flops 40960 | bytes 245760 | tf_op jit(solution)/shard_map/psum | solution.py:200
  275.5 1.3 fusion.85
  276.9 10.0 %all-gather.5.cloned.1.call-done = bf16[1280,2560]{1,0:T(8,128)(2,1)} async-done(((bf16[1280,640]{1,0:T(8,128)(2,1)}), bf16[1280,2560]{1,0:T(8,128)(2,1)}) %all-gather.5.cloned.1.call-update) | async-done | bytes 6553616 | tf_op jit(solution)/shard_map/all_gather | solution.py:155
  286.8 5.7 %fusion.84 = f32[512,2560]{1,0:T(8,128)S(1)} fusion(bf16[512,1280]{1,0:T(8,128)(2,1)S(1)} %fusion.52, bf16[1280,2560]{1,0:T(8,128)(2,1)} %all-gather.5.cloned.1.call-done), kind=kOutput, calls=%fused_computation.121 | convolution fusion | flops 3355443200 | bytes 13107200 | tf_op jit(solution)/shard_map/dot_general | solution.py:165
  292.5 2.4 multiply_convert_fusion
  295.0 38.2 %all-reduce.8.cloned.1.call-done = bf16[16,2560]{1,0:T(8,128)(2,1)} async-done(((bf16[16,2560]{1,0:T(8,128)(2,1)}), bf16[16,2560]{1,0:T(8,128)(2,1)}) %all-reduce.8.cloned.1.call-update) | async-done | bytes 81936 | tf_op jit(solution)/shard_map/psum | solution.py:201
  333.1 1.6 convert_element_type.128
  334.7 54.9 %all-reduce.6.cloned.1.call-done = f32[1280,16]{0,1:T(8,128)} async-done(((f32[1280,16]{0,1:T(8,128)}), f32[1280,16]{0,1:T(8,128)}) %all-reduce.6.cloned.1.call-update) | async-done | bytes 81936 | tf_op jit(solution)/shard_map/psum | solution.py:200
  389.6 43.9 %reduce-scatter.2.cloned.1.call-done = bf16[128,2560]{1,0:T(8,128)(2,1)} async-done(((bf16[512,2560]{1,0:T(8,128)(2,1)}), bf16[128,2560]{1,0:T(8,128)(2,1)}) %reduce-scatter.2.cloned.1.call-update) | async-done | bytes 655376 | tf_op jit(solution)/shard_map/reduce_scatter | solution.py:175
  433.5 1.5 copy.140
  (123 shorter events, 5.7 us)
Async XLA Ops:
  7.2 211.3 %copy-start = (bf16[1,128,2560]{2,1,0:T(8,128)(2,1)S(1)}, bf16[1,128,2560]{2,1,0:T(8,128)(2,1)}, u32[]{:S(2)}) copy-start(bf16[1,128,2560]{2,1,0:T(8,128)(2,1)} %param.29) | copy-start | bytes 1966084
  7.2 12.2 %copy-start.5 = (bf16[1,128,5120]{2,1,0:T(8,128)(2,1)S(1)}, bf16[1,128,5120]{2,1,0:T(8,128)(2,1)}, u32[]{:S(2)}) copy-start(bf16[1,128,5120]{2,1,0:T(8,128)(2,1)} %param.16) | copy-start | bytes 3932164
  7.2 12.2 %copy-start.11 = (bf16[1,128,256]{2,1,0:T(8,128)(2,1)S(1)}, bf16[1,128,256]{2,1,0:T(8,128)(2,1)}, u32[]{:S(2)}) copy-start(bf16[1,128,256]{2,1,0:T(8,128)(2,1)} %param.17) | copy-start | bytes 196612
  7.2 12.2 %copy-start.18 = (f32[5376]{0:T(1024)S(1)}, f32[5376]{0:T(1024)}, u32[]{:S(2)}) copy-start(f32[5376]{0:T(1024)} %param.21) | copy-start | bytes 64516
  8.3 9.4 %collective-permute-start = (bf16[3,5376]{1,0:T(4,128)(2,1)S(1)}, bf16[3,5376]{1,0:T(4,128)(2,1)S(1)}, u32[]{:S(2)}, u32[]{:S(2)}) collective-permute-start(bf16[3,5376]{1,0:T(4,128)(2,1)S(1)} %fusion.75), channel_id=1, source_target_pairs={{0,4},{4,8},{8,12},{12,16},{16,20},{20,24},{24,28},{1,5},{5,9},{9,... | collective-permute-start | bytes 96776 | tf_op jit(solution)/shard_map/ppermute | solution.py:14
  13.0 10.1 %all-to-all-start = ((bf16[128,4,20]{0,2,1:T(8,128)(2,1)}), bf16[128,4,20]{0,2,1:T(8,128)(2,1)S(1)}, u32[]{:S(2)}, u32[]{:S(2)}) async-start(bf16[128,4,20]{0,2,1:T(8,128)(2,1)} %all_to_all.30), calls=%async_computation | async-start | bytes 49152 | tf_op jit(solution)/shard_map/all_to_all | solution.py:123
  21.6 5.7 %copy-start.21 = (f32[20]{0:T(128)S(1)}, f32[20]{0:T(128)}, u32[]{:S(2)}) copy-start(f32[20]{0:T(128)} %param.23) | copy-start | bytes 244
  21.6 6.4 %copy-start.20 = (f32[20]{0:T(128)S(1)}, f32[20]{0:T(128)}, u32[]{:S(2)}) copy-start(f32[20]{0:T(128)} %param.22) | copy-start | bytes 244
  23.1 4.2 copy-start.15
  23.1 26.3 %all-to-all-start.1 = ((bf16[128,4,1280]{0,2,1:T(8,128)(2,1)}), bf16[128,4,1280]{0,2,1:T(8,128)(2,1)S(1)}, u32[]{:S(2)}, u32[]{:S(2)}) async-start(bf16[128,4,1280]{0,2,1:T(8,128)(2,1)} %bitcast.3), calls=%async_computation.1 | async-start | bytes 2621440 | tf_op jit(solution)/shard_map/all_to_all | solution.py:119
  27.3 163.0 %all-gather.7.cloned.1.call-start = ((), (), s32[]{:S(2)}) async-start(), calls=%async_computation.8 | async-start | bytes 1966080 | tf_op jit(solution)/shard_map/all_gather | solution.py:19
  27.3 0.6 copy-start.12
  48.0 0.7 copy-start.9
  55.1 3.4 copy-start.1
  61.6 9.1 %copy-start.7 = (f32[1,256,20]{1,2,0:T(8,128)}, f32[1,256,20]{1,2,0:T(8,128)S(1)}, u32[]{:S(2)}) copy-start(f32[1,256,20]{1,2,0:T(8,128)S(1)} %copy.123) | copy-start | bytes 61444 | tf_op jit(solution)/shard_map/while
  108.0 9.1 %copy-start.7 = (f32[1,256,20]{1,2,0:T(8,128)}, f32[1,256,20]{1,2,0:T(8,128)S(1)}, u32[]{:S(2)}) copy-start(f32[1,256,20]{1,2,0:T(8,128)S(1)} %copy.123) | copy-start | bytes 61444 | tf_op jit(solution)/shard_map/while
  152.0 1.3 copy-start.8
  152.0 134.8 %all-gather.5.cloned.1.call-start = ((), (), s32[]{:S(2)}) async-start(), calls=%async_computation.4 | async-start | bytes 8192000 | tf_op jit(solution)/shard_map/all_gather | solution.py:155
  153.3 5.1 %copy-start.23 = (u32[32]{0:T(128)S(1)}, u32[32]{0:T(128)}, u32[]{:S(2)}) copy-start(u32[32]{0:T(128)} %constant.76) | copy-start | bytes 388
  153.3 6.3 %copy-start.13 = (f32[4,128,20]{1,2,0:T(8,128)S(1)}, f32[4,128,20]{1,2,0:T(8,128)}, u32[]{:S(2)}) copy-start(f32[4,128,20]{1,2,0:T(8,128)} %copy-done.12) | copy-start | bytes 122884
  153.3 8.9 %copy-start.16 = (bf16[128,4,20]{0,2,1:T(8,128)(2,1)S(1)}, bf16[128,4,20]{0,2,1:T(8,128)(2,1)}, u32[]{:S(2)}) copy-start(bf16[128,4,20]{0,2,1:T(8,128)(2,1)} %copy-done.15) | copy-start | bytes 61444
  154.8 17.3 %all-to-all-start.2 = ((bf16[128,4,1280]{0,2,1:T(8,128)(2,1)}), bf16[128,4,1280]{0,2,1:T(8,128)(2,1)S(1)}, u32[]{:S(2)}, u32[]{:S(2)}) async-start(bf16[128,4,1280]{0,2,1:T(8,128)(2,1)} %bitcast.12), calls=%async_computation.2 | async-start | bytes 2621440 | tf_op jit(solution)/shard_map/all_to_all | solution.py:122
  158.3 174.8 %all-reduce.8.cloned.1.call-start = ((), (), s32[]{:S(2)}) async-start(), calls=%async_computation.7 | async-start | bytes 163840 | tf_op jit(solution)/shard_map/psum | solution.py:201
  172.7 2.0 copy-start.3
  178.9 4.3 copy-start.2
  185.3 4.9 %copy-start.6 = (f32[512,20,64]{0,2,1:T(8,128)S(1)}, f32[512,20,64]{0,2,1:T(8,128)}, u32[]{:S(2)}) copy-start(f32[512,20,64]{0,2,1:T(8,128)} %reshape.166) | copy-start | bytes 7864324
  185.3 4.9 %copy-start.10 = (bf16[512,256]{1,0:T(8,128)(2,1)S(1)}, bf16[512,256]{1,0:T(8,128)(2,1)}, u32[]{:S(2)}) copy-start(bf16[512,256]{1,0:T(8,128)(2,1)} %copy-done.9) | copy-start | bytes 786436
  185.3 4.9 %copy-start.22 = (f32[20]{0:T(128)S(1)}, f32[20]{0:T(128)}, u32[]{:S(2)}) copy-start(f32[20]{0:T(128)} %param.24) | copy-start | bytes 244
  196.6 3.4 copy-start.4
  196.6 3.4 copy-start.19
  200.0 2.7 copy-start.17
  200.0 18.9 %copy-start.14 = (bf16[16,2560]{1,0:T(8,128)(2,1)S(1)}, bf16[16,2560]{1,0:T(8,128)(2,1)}, u32[]{:S(2)}) copy-start(bf16[16,2560]{1,0:T(8,128)(2,1)} %param.28) | copy-start | bytes 245764
  275.5 114.1 %all-reduce.6.cloned.1.call-start = ((), (), s32[]{:S(2)}) async-start(), calls=%async_computation.6 | async-start | bytes 163840 | tf_op jit(solution)/shard_map/psum | solution.py:200
  276.8 156.7 %reduce-scatter.2.cloned.1.call-start = ((), (), s32[]{:S(2)}) async-start(), calls=%async_computation.5 | async-start | bytes 3276800 | tf_op jit(solution)/shard_map/reduce_scatter | solution.py:175
Sparse Core Ops, SparseCore 0:
  152.1 9.6 all-gather.6
  163.4 123.3 all-gather.4
  290.3 42.7 all-reduce.7
  335.9 53.6 all-reduce.5
  393.0 40.4 reduce-scatter.1
where the time goes:
time: 448 us; the launch traced here: 442 us
  waiting for transfers between devices  155 us (35%)
  local copies, waits for them, and re-layouts  105 us (23%)
  blocking collectives  93.2 us (21%)
  matrix products  41.7 us (9%)
  other arithmetic  17.5 us (4%)
  between operations  14.8 us (3%)
  starting transfers between devices  14.5 us (3%)
    dynamic_update_slice x4, local copies, waits for them, and re-layouts, ssd_blocks(): lax.scan(advance, start_state, (x_heads.reshape(blocks, block_len, head_c...  56.8 us
    psum x1, waiting for transfers between devices, shards(): lax.psum((grad_a_local, grad_b_local), ('context', 'fsdp'))  54.9 us
    psum x1, blocking collectives, shards(): lax.psum((grad_a_local, grad_b_local), ('context', 'fsdp'))  48.1 us
    reduce_scatter x1, waiting for transfers between devices, shards(): lax.psum_scatter((row_slice(scale_all, start_row, lax.axis_size('tensor')...  43.9 us
    psum x1, waiting for transfers between devices, shards(): lax.psum(grad_b_part.astype(jnp.bfloat16), 'tensor').astype(jnp.float32)  38.2 us
    all_gather x1, blocking collectives, shards(): lax.all_gather(convolved[:, inner_width:], 'tensor', axis=0, tiled=True)  19.2 us
    psum x1, blocking collectives, shards(): lax.psum(adapter_piece.astype(jnp.bfloat16), 'tensor').astype(jnp.float32)  15.3 us
    dot_general x2, matrix products, advance(): jnp.einsum('hij,jhp->ihp', decay_mat * gram_mat[None], x_scaled, precisio...  11.9 us
  transfers between devices with their start and end apart: 9, of which 5 were waited for; matrix products, arithmetic and copies ran while one was open for 13% of the time, Pallas kernels for 0%

commit v1 on v0

v1 whole, which is shorter than its diff:
```python
import functools
import math

import jax
import jax.numpy as jnp
from jax import lax
from jax.experimental import pallas as pl
from jax.experimental.pallas import tpu as pltpu
from jax.sharding import PartitionSpec as P

EPS = 1e-05
MESH = pl.DeviceIdType.MESH
HI = lax.Precision.HIGHEST
BF = jnp.bfloat16
F32 = jnp.float32


def dot(a, b, ca=1, cb=0, precision=None):
    return lax.dot_general(
        a, b, (((ca,), (cb,)), ((), ())), preferred_element_type=F32, precision=precision
    )


def iota(shape, dim):
    return lax.broadcasted_iota(jnp.int32, shape, dim)


def kernel(
    nt, nf, nc, hl,
    x_ref, bc_ref, z_ref, dt_ref, taps_ref, bias_ref, hp_ref, gain_ref, w_ref, down_ref, up_ref, cot_ref,
    mixed_ref, ga_ref, gb_ref,
    halo_x, halo_bc, x_send, x_all, z_all, bc_all, dt_all, wbuf, a_s, step_s, at_s, stept_s,
    stl, msg, st_in, inc_s, e_s, y_s, g_s, adx, ad_in, ag_own, ag_all, gb_own, gb_in, comb, comb_c, comb2, comb_f,
    fin, rs_send, rs_recv,
    h_ss, h_rs, dt_ss, dt_rs, bc_ss, bc_rs, x_ss, x_rs, z_ss, z_rs, w_ss, w_rs, wf_ss, wf_rs, st_ss, st_rs,
    ad_ss, ad_rs, ag_ss, ag_rs, ga_ss, ga_rs, cc_ss, cc_rs, cf_ss, cf_rs, fin_ss, fin_rs, r_ss, r_rs, loc,
):
    t = lax.axis_index("tensor")
    f = lax.axis_index("fsdp")
    c = lax.axis_index("context")
    L = x_ref.shape[0]
    LW = x_all.shape[1]
    W = w_ref.shape[1]
    N = bc_ref.shape[1] // 2
    R = w_ref.shape[0] // nc
    HS = LW // hl
    idx = c * nt + t
    total = nc * nt

    def tp(e):
        return lax.rem(t + e, nt)

    def place(i):
        return {"context": i // nt, "tensor": lax.rem(i, nt)}

    def copy(src, dst, ss, rs, dev):
        cp = pltpu.make_async_remote_copy(
            src_ref=src, dst_ref=dst, send_sem=ss, recv_sem=rs, device_id=dev, device_id_type=MESH
        )
        cp.start()
        return cp

    nxt, prv = lax.rem(idx + 1, total), lax.rem(idx + total - 1, total)
    bar = pltpu.get_barrier_semaphore()
    greet = [{"tensor": tp(e)} for e in range(1, nt)]
    greet += [{"fsdp": lax.rem(f + d, nf)} for d in range(1, nf)]
    greet += [{"context": lax.rem(c + k, nc)} for k in range(1, nc)]
    greet += [place(nxt), place(prv)]
    for dev in greet:
        pl.semaphore_signal(bar, inc=1, device_id=dev, device_id_type=MESH)
    pl.semaphore_wait(bar, len(greet))
    sent = []

    h1 = copy(x_ref.at[L - 16 : L, :], halo_x, h_ss.at[0], h_rs.at[0], place(nxt))
    h2 = copy(bc_ref.at[L - 16 : L, :], halo_bc, h_ss.at[1], h_rs.at[1], place(nxt))
    own_rows = pl.ds(pl.multiple_of(t * L, L), L)
    dts = [copy(dt_ref, dt_all.at[own_rows, :], dt_ss.at[e], dt_rs.at[e], {"tensor": tp(e)}) for e in range(1, nt)]
    share = pl.ds(pl.multiple_of(c * R, 16), R)
    ws = [
        copy(w_ref.at[share, :], wbuf.at[d, share, :], w_ss.at[d], w_rs.at[d], {"fsdp": lax.rem(f + d, nf)})
        for d in range(1, nf)
    ]
    own_w = pltpu.make_async_copy(w_ref, wbuf.at[0], loc.at[0])
    own_w.start()
    own_cols = pl.ds(pl.multiple_of(t * LW, 128), LW)
    own_z = pltpu.make_async_copy(z_ref.at[:, own_cols], z_all.at[own_rows, :], loc.at[1])
    own_z.start()
    dt_all[own_rows, :] = dt_ref[...]

    h1.wait()
    h2.wait()
    live = (idx > 0).astype(F32)

    def conv(src, halo, col, tap_col):
        lanes = pl.ds(col, 128)
        wide = pl.ds(tap_col, 128)
        ext = jnp.concatenate([halo[8:16, lanes].astype(F32) * live, src[:, lanes].astype(F32)], axis=0)
        acc = bias_ref[:, wide] + taps_ref[0:1, wide] * ext[5 : 5 + L]
        for k in range(1, 4):
            acc = acc + taps_ref[k : k + 1, wide] * ext[5 + k : 5 + k + L]
        return (acc / (1.0 + jnp.exp(-acc))).astype(BF)

    wide0 = x_ref.shape[1]
    for j in range(2 * N // 128):
        bc_all[own_rows, j * 128 : (j + 1) * 128] = conv(bc_ref, halo_bc, j * 128, wide0 + j * 128)
    bcs = [
        copy(bc_all.at[own_rows, :], bc_all.at[own_rows, :], bc_ss.at[e], bc_rs.at[e], {"tensor": tp(e)})
        for e in range(1, nt)
    ]
    xs, zs = [], []

    def conv_group(e, store):
        base = tp(e) * LW

        def lap(j, carry):
            col = pl.multiple_of(base + j * 128, 128)
            store(pl.ds(pl.multiple_of(j * 128, 128), 128), conv(x_ref, halo_x, col, col))
            return carry

        lax.fori_loop(0, LW // 128, lap, 0)

    for e in range(1, nt):
        def put(lanes, val, e=e):
            x_send[e - 1, :, lanes] = val

        conv_group(e, put)
        xs.append(copy(x_send.at[e - 1], x_all.at[own_rows, :], x_ss.at[e], x_rs.at[e], {"tensor": tp(e)}))
    for e in range(1, nt):
        cols = pl.ds(pl.multiple_of(tp(e) * LW, 128), LW)
        zs.append(copy(z_ref.at[:, cols], z_all.at[own_rows, :], z_ss.at[e], z_rs.at[e], {"tensor": tp(e)}))

    def put_own(lanes, val):
        x_all[own_rows, lanes] = val

    conv_group(0, put_own)
    e_s[...] = (iota((128, LW), 1) // HS == iota((128, LW), 0)).astype(F32)
    spread16 = e_s[...].astype(BF)

    def spread(rows):
        return dot(jnp.broadcast_to(rows, (8, 128)), e_s[...], precision=HI)

    for cp in dts:
        cp.wait()
    HR = at_s.shape[1]
    sel = ((iota((128, 128), 0) == iota((128, 128), 1) + t * hl) & (iota((128, 128), 1) < hl)).astype(BF)
    sel_t = ((iota((HR, 128), 1) == iota((HR, 128), 0) + t * hl) & (iota((HR, 128), 0) < hl)).astype(BF)
    eye = (iota((HR, 128), 0) == iota((HR, 128), 1)).astype(F32)
    hp = hp_ref[...]
    hp_t = dot(eye, hp, 1, 1, HI)
    tri = (iota((L, L), 0) >= iota((L, L), 1)).astype(F32)

    def softplus(v):
        return jnp.maximum(v, 0.0) + jnp.log1p(jnp.exp(-jnp.abs(v)))

    for b in range(nt):
        rows = slice(b * L, (b + 1) * L)
        raw = dt_all[rows, :]
        step = softplus(dot(raw, sel) + hp[0:1, :])
        step_s[rows, :] = step
        a_s[rows, :] = dot(tri, -step * jnp.exp(hp[1:2, :]), precision=HI)
        step_t = softplus(dot(sel_t, raw, 1, 1) + hp_t[:, 0:1])
        stept_s[b] = step_t
        at_s[b] = dot(-step_t * jnp.exp(hp_t[:, 1:2]), tri, 1, 1, HI)
    for cp in bcs:
        cp.wait()
    for cp in xs:
        cp.wait()

    state = jnp.zeros((N, LW), F32)
    before = jnp.zeros((1, 128), F32)
    for b in range(nt):
        rows = slice(b * L, (b + 1) * L)
        stl[b, 0:N, :] = state
        stl[b, N : N + 8, :] = spread(jnp.exp(before))
        a = a_s[rows, :]
        last = a[L - 1 : L, :]
        weight = (jnp.exp(last - a) * step_s[rows, :]).astype(BF)
        xw = (x_all[rows, :].astype(F32) * dot(weight, spread16)).astype(BF)
        state = spread(jnp.exp(last))[0:1, :] * state + dot(bc_all[rows, 0:N], xw, 0, 0)
        before = before + last
    msg[0:N, :] = state
    msg[N : N + 8, :] = spread(before)
    sts = [
        copy(msg, st_in.at[c], st_ss.at[k], st_rs.at[k], {"context": lax.rem(c + k, nc)})
        for k in range(1, nc)
    ]

    left = iota((L, 2 * HS), 1) < HS

    def inner(b, carry):
        rows = pl.ds(pl.multiple_of(b * L, L), L)
        gram = dot(bc_all[rows, N : 2 * N], bc_all[rows, 0:N], 1, 1)
        gram = jnp.where(iota((L, L), 0) >= iota((L, L), 1), gram, 0.0)
        a = a_s[rows, :]
        at = at_s[b]
        stt = stept_s[b]
        for pair in range(hl // 2):
            lanes = slice(pair * 2 * HS, (pair + 1) * 2 * HS)
            xp = x_all[rows, lanes]
            out = []
            for h in (2 * pair, 2 * pair + 1):
                gap = jnp.minimum(a[:, h : h + 1] - at[h : h + 1, :], 0.0)
                m = (jnp.exp(gap) * gram * stt[h : h + 1, :]).astype(BF)
                out.append(dot(m, xp))
            y_s[rows, lanes] = jnp.where(left, out[0], out[1])
        return carry

    lax.fori_loop(0, nt, inner, 0)

    for cp in sts:
        cp.wait()
    inc_s[...] = jnp.zeros_like(inc_s)

    def chain(k, carry):
        inc_s[...] = jnp.exp(st_in[k, N : N + 1, :]) * inc_s[...] + st_in[k, 0:N, :]
        return carry

    lax.fori_loop(0, c, chain, 0)
    for cp in zs:
        cp.wait()
    own_z.wait()
    skip = spread(hp[2:3, :])[0:1, :]
    ones = jnp.ones((8, LW), BF)

    def gate(b, carry):
        rows = pl.ds(pl.multiple_of(b * L, L), L)
        start = (stl[b, 0:N, :] + stl[b, N : N + 1, :] * inc_s[...]).astype(BF)
        reach = dot(jnp.exp(a_s[rows, :]).astype(BF), spread16)
        y = y_s[rows, :] + reach * dot(bc_all[rows, N : 2 * N], start)
        y = y + skip * x_all[rows, :].astype(F32)
        z = z_all[rows, :].astype(F32)
        g = y * (z / (1.0 + jnp.exp(-z)))
        out = (g * gain_ref[...]).astype(BF)
        g_s[rows, :] = out
        adx[b, 0:16, :] = dot(down_ref[...], out, 1, 1)
        adx[b, 16:24, :] = dot(ones, (g * g).astype(BF), 1, 1)
        return carry

    lax.fori_loop(0, nt, gate, 0)
    ads = [copy(adx.at[tp(e)], ad_in.at[e], ad_ss.at[e], ad_rs.at[e], {"tensor": tp(e)}) for e in range(1, nt)]

    half = (nt * L) // 2

    def project(d):
        def lap(i, carry):
            rows = pl.ds(pl.multiple_of(i * half, half), half)
            rs_send[d, rows, :] = dot(g_s[rows, :], wbuf[d]).astype(BF)
            return carry

        lax.fori_loop(0, 2, lap, 0)

    def scatter(d):
        return [
            copy(
                rs_send.at[d, pl.ds(pl.multiple_of(tp(e) * L, L), L), :],
                rs_recv.at[d, e - 1], r_ss.at[d, e], r_rs.at[d, e], {"tensor": tp(e)},
            )
            for e in range(1, nt)
        ]

    own_w.wait()
    project(0)
    for cp in ads:
        cp.wait()
    red = adx[t]
    for e in range(1, nt):
        red = red + ad_in[e]
    scale_row = lax.rsqrt(red[16:17, :] / (LW * nt) + EPS)
    ad16 = red[0:16, :].astype(BF)
    factor = 2.0 / math.sqrt(L * nt * nc * nf)
    cot = cot_ref[...]
    ag_own[...] = factor * scale_row * dot(up_ref[...], cot, 1, 1)
    ags = [copy(ag_own, ag_all.at[t], ag_ss.at[e], ag_rs.at[e], {"tensor": tp(e)}) for e in range(1, nt)]
    gb_own[...] = dot((factor * scale_row * ad16.astype(F32)).astype(BF), cot)
    part = gb_own.shape[1] // nt
    own_part = pl.ds(pl.multiple_of(t * part, 128), part)
    gbs = [
        copy(
            gb_own.at[:, pl.ds(pl.multiple_of(tp(e) * part, 128), part)],
            gb_in.at[e], ga_ss.at[e], ga_rs.at[e], {"tensor": tp(e)},
        )
        for e in range(1, nt)
    ]
    sent += scatter(0)
    wfs = []
    for d in range(1, nf):
        ws[d - 1].wait()
        wfs.append([
            copy(wbuf.at[d, share, :], wbuf.at[d, share, :], wf_ss.at[d, k], wf_rs.at[d, k], {"context": lax.rem(c + k, nc)})
            for k in range(1, nc)
        ])
    for d in range(1, 2):
        for cp in wfs[d - 1]:
            cp.wait()
        project(d)
        sent += scatter(d)
    for cp in ags + gbs:
        cp.wait()
    ag_all[t] = ag_own[...]
    grad = jnp.zeros((16, LW), F32)
    for s in range(nt):
        grad = grad + dot(ag_all[s].astype(BF), g_s[s * L : (s + 1) * L, :])
    comb[:, 0:LW] = grad
    acc = gb_own[:, own_part]
    for e in range(1, nt):
        acc = acc + gb_in[e]
    comb[:, LW : LW + part] = acc
    ccs = [copy(comb, comb_c.at[k], cc_ss.at[k], cc_rs.at[k], {"context": lax.rem(c + k, nc)}) for k in range(1, nc)]
    for d in range(2, nf):
        for cp in wfs[d - 1]:
            cp.wait()
        project(d)
        sent += scatter(d)
        if d == 2:
            for cp in ccs:
                cp.wait()
            acc = comb[...]
            for k in range(1, nc):
                acc = acc + comb_c[k]
            comb2[...] = acc
            cfs = [copy(comb2, comb_f.at[k], cf_ss.at[k], cf_rs.at[k], {"fsdp": lax.rem(f + k, nf)}) for k in range(1, nf)]
    for cp in cfs:
        cp.wait()
    acc = comb2[...]
    for k in range(1, nf):
        acc = acc + comb_f[k]
    ga_ref[...] = acc[:, 0:LW]
    fin[t] = acc[:, LW:]
    fins = [copy(fin.at[t], fin.at[t], fin_ss.at[e], fin_rs.at[e], {"tensor": tp(e)}) for e in range(1, nt)]
    scale_col = dot(jnp.broadcast_to(scale_row, (8, L)), jnp.full((8, 128), 0.125, F32), 0, 0, HI)[:, 0:1]
    for d in range(nf):
        for cp in sent[d * (nt - 1) : (d + 1) * (nt - 1)]:
            cp.wait()
        cols = pl.ds(pl.multiple_of(lax.rem(f + nf - d, nf) * W, 128), W)
        acc = rs_send[d, own_rows, :].astype(F32)
        for e in range(1, nt):
            acc = acc + rs_recv[d, e - 1].astype(F32)
        acc = acc + 2.0 * dot(ad16, up_ref[:, cols], 0, 0)
        mixed_ref[:, cols] = (scale_col * acc).astype(BF)
    for cp in fins:
        cp.wait()
    for s in range(nt):
        gb_ref[:, s * part : (s + 1) * part] = fin[s]


def shards(x, bc, z, dt, taps, bias, step_bias, rate, skip, gain, w, down, up, cot):
    nt, nf, nc = lax.axis_size("tensor"), lax.axis_size("fsdp"), lax.axis_size("context")
    L, full = x.shape[1], x.shape[2]
    LW, hl, W, M = gain.shape[0], step_bias.shape[0], w.shape[1], cot.shape[2]
    BC = bc.shape[2]
    N = BC // 2
    HR = -(-hl // 8) * 8
    T = nt * L
    part = M // nt
    hp = jnp.pad(jnp.stack([step_bias, rate, skip]), ((0, 5), (0, 128 - hl)))
    dt = jnp.pad(dt[0], ((0, 0), (0, 128 - dt.shape[2])))
    vm = pl.BlockSpec(memory_space=pltpu.VMEM)
    hbm = pl.BlockSpec(memory_space=pl.ANY)
    V = pltpu.VMEM
    D = pltpu.SemaphoreType.DMA
    scratch = [
        V((16, full), BF), V((16, BC), BF), V((nt - 1, L, LW), BF), V((T, LW), BF), V((T, LW), BF),
        V((T, BC), BF), V((T, 128), BF), V((nf, LW, W), BF), V((T, 128), F32), V((T, 128), F32),
        V((nt, HR, L), F32), V((nt, HR, L), F32),
        V((nt, N + 8, LW), F32), V((N + 8, LW), F32), V((nc, N + 8, LW), F32), V((N, LW), F32),
        V((128, LW), F32), V((T, LW), F32), V((T, LW), BF), V((nt, 24, L), F32), V((nt, 24, L), F32),
        V((16, L), F32), V((nt, 16, L), F32), V((16, M), F32), V((nt, 16, part), F32),
        V((16, LW + part), F32), V((nc, 16, LW + part), F32), V((16, LW + part), F32), V((nf, 16, LW + part), F32),
        V((nt, 16, part), F32), V((nf, T, W), BF), V((nf, nt - 1, L, W), BF),
        D((2,)), D((2,)), D((nt,)), D((nt,)), D((nt,)), D((nt,)), D((nt,)), D((nt,)), D((nt,)), D((nt,)),
        D((nf,)), D((nf,)), D((nf, nc)), D((nf, nc)), D((nc,)), D((nc,)),
        D((nt,)), D((nt,)), D((nt,)), D((nt,)), D((nt,)), D((nt,)), D((nc,)), D((nc,)), D((nf,)), D((nf,)),
        D((nt,)), D((nt,)), D((nf, nt)), D((nf, nt)), D((2,)),
    ]
    mixed, ga, gb = pl.pallas_call(
        functools.partial(kernel, nt, nf, nc, hl),
        out_shape=(
            jax.ShapeDtypeStruct((L, M), BF),
            jax.ShapeDtypeStruct((16, LW), F32),
            jax.ShapeDtypeStruct((16, M), F32),
        ),
        in_specs=[vm, vm, hbm, vm, vm, vm, vm, vm, hbm, vm, vm, vm],
        out_specs=(vm, vm, vm),
        scratch_shapes=scratch,
        compiler_params=pltpu.CompilerParams(
            collective_id=0, has_side_effects=True, vmem_limit_bytes=62 * 1024 * 1024
        ),
    )(x[0], bc[0], z[0], dt, taps, bias[None], hp, gain[None], w, down.T, up, cot[0])
    return mixed[None], ga.T, gb


def solution(mesh):
    tokens = P("fsdp", ("context", "tensor"), None)
    placed = (
        tokens, tokens, tokens, tokens, P(), P(), P("tensor"), P("tensor"), P("tensor"), P("tensor"),
        P("tensor", "fsdp"), P("tensor", None), P(), tokens,
    )
    return jax.shard_map(
        shards, mesh=mesh, in_specs=placed, out_specs=(tokens, P("tensor", None), P()), check_vma=False
    )
```

time: 448 us -> 119 us (0.27); the launches traced: 442 us -> 118 us
  waiting for transfers between devices: 155 us -> 0 us
  Pallas kernels: 0 us -> 109 us
  local copies, waits for them, and re-layouts: 105 us -> 7.43 us
  blocking collectives: 93.2 us -> 0 us
  matrix products: 41.7 us -> 0 us
  other arithmetic: 17.5 us -> 1.29 us
  starting transfers between devices: 14.5 us -> 0 us
  between operations: 14.8 us -> 0.66 us
    pallas_call x0 -> x1, Pallas kernels: none -> 109 us  [shards(): pl.pallas_call(functools.partial(kernel, nt, nf, nc, hl), out_shape=(jax....]
    psum x2 -> x0, waiting for transfers between devices: 93.1 us -> none  [the longest x1 54.9 us: shards(): lax.psum((grad_a_local, grad_b_local), ('context', 'fsdp'))]
    psum x2 -> x0, blocking collectives: 63.4 us -> none  [the longest x1 48.1 us: shards(): lax.psum((grad_a_local, grad_b_local), ('context', 'fsdp'))]
    dynamic_update_slice x4 -> x0, local copies, waits for them, and re-layouts: 56.8 us -> none  [ssd_blocks(): lax.scan(advance, start_state, (x_heads.reshape(blocks, block_len, head_c...]
    reduce_scatter x1 -> x0, waiting for transfers between devices: 43.9 us -> none  [shards(): lax.psum_scatter((row_slice(scale_all, start_row, lax.axis_size('tensor')...]
    dot_general x15 -> x0, matrix products: 41.7 us -> none  [the longest x2 11.9 us: advance(): jnp.einsum('hij,jhp->ihp', decay_mat * gram_mat[None], x_scaled, precisio...]
    all_gather x2 -> x0, blocking collectives: 27.3 us -> none  [the longest x1 19.2 us: shards(): lax.all_gather(convolved[:, inner_width:], 'tensor', axis=0, tiled=True)]
    convert_element_type x8 -> x0, local copies, waits for them, and re-layouts: 19.5 us -> none  [the longest x3 10.9 us: shards(): x_heads_raw.astype(jnp.float32).reshape(span_rows, local_heads, head_size)]
  transfers between devices with their start and end apart: 9 -> 0, of which waited for: 5 -> 0; matrix products, arithmetic and copies ran while one was open for 13% -> 0% of each run, Pallas kernels for 0% -> 0%
where the time goes in v1:
time: 119 us; the launch traced here: 118 us
  Pallas kernels  109 us (92%)
  local copies, waits for them, and re-layouts  7.43 us (6%)
  other arithmetic  1.29 us (1%)
    pallas_call x1, Pallas kernels, shards(): pl.pallas_call(functools.partial(kernel, nt, nf, nc, hl), out_shape=(jax....  109 us
    unnamed x8, local copies, waits for them, and re-layouts  4.15 us

profile of v1, /device:TPU:24, one launch (start us, length us, event | category | flops | bytes accessed | tf_op | source)
XLA Modules:
  0.0 118.4 jit_solution(12969904934923448778)
XLA Ops:
  0.6 1.3 %select_maximum_fusion.hp_ref = f32[8,128]{1,0:T(8,128)} fusion(f32[1,20]{1,0:T(1,128)} %bitcast.19, f32[1,20]{1,0:T(1,128)} %bitcast.20, f32[1,20]{1,0:T(1,128)} %bitcast.21), kind=kLoop, calls=%fused_computation | loop fusion | flops 11264 | bytes 4336 | tf_op jit(solution)/shard_map/stack | solution.py:355
  1.9 1.3 %broadcast_in_dim.10.gain_ref = f32[1,1280]{1,0:T(1,128)} reshape(f32[1280]{0:T(1024)} %param.23) | data formatting | bytes 10240 | tf_op jit(solution)/shard_map/broadcast_in_dim | solution.py:388
  3.2 1.4 %broadcast_in_dim.9.bias_ref = f32[1,5376]{1,0:T(1,128)} reshape(f32[5376]{0:T(1024)} %param.19) | data formatting | bytes 43008 | tf_op jit(solution)/shard_map/broadcast_in_dim | solution.py:388
  4.6 0.8 copy.17
  5.4 0.6 pad.8.dt_ref
  6.0 109.0 %shard_map.157 = (bf16[128,2560]{1,0:T(8,128)(2,1)}, f32[16,1280]{1,0:T(8,128)}, f32[16,2560]{1,0:T(8,128)}) custom-call(bf16[128,5120]{1,0:T(8,128)(2,1)} %bitcast.11, bf16[128,256]{1,0:T(8,128)(2,1)} %bitcast.17, bf16[128,5120]{1,0:T(8,128)(2,1)} %bitcast.12, bf16[128,128]{1,0:T(8,128)(2,1)} %pad.8.dt_ref, f32[4,5376]{1,0:T(4,128)} %taps_ref.1, ...), custom_call_target="tpu_custom_call" | custom-call | tf_op jit(solution)/shard_map/pallas_call | solution.py:375
  115.0 0.0 copy-start.1
  115.0 0.0 copy-start
  115.0 2.0 %copy.21 = bf16[1,128,2560]{2,1,0:T(8,128)(2,1)} copy(bf16[1,128,2560]{2,1,0:T(8,128)(2,1)} %bitcast.14) | data formatting | bytes 1310720
  117.1 0.0 copy-done.1
  117.1 0.6 copy.22
  117.7 0.0 copy-done
  117.7 0.7 copy.23
Async XLA Ops:
  115.0 2.0 %copy-start.1 = (f32[16,1280]{1,0:T(8,128)S(1)}, f32[16,1280]{1,0:T(8,128)}, u32[]{:S(2)}) copy-start(f32[16,1280]{1,0:T(8,128)} %get-tuple-element.7) | copy-start | bytes 245764
  115.0 2.7 %copy-start = (f32[16,2560]{1,0:T(8,128)S(1)}, f32[16,2560]{1,0:T(8,128)}, u32[]{:S(2)}) copy-start(f32[16,2560]{1,0:T(8,128)} %get-tuple-element.14) | copy-start | bytes 491524

commit v2 on v1

--- a/solution.py
+++ b/solution.py
@@ -27,7 +27,7 @@
 
 def kernel(
     nt, nf, nc, hl,
-    x_ref, bc_ref, z_ref, dt_ref, taps_ref, bias_ref, hp_ref, gain_ref, w_ref, down_ref, up_ref, cot_ref,
+    x_ref, bc_ref, z_ref, dt_ref, taps_ref, bias_ref, sb_ref, dr_ref, sk_ref, gain_ref, w_ref, down_ref, up_ref, cot_ref,
     mixed_ref, ga_ref, gb_ref,
     halo_x, halo_bc, x_send, x_all, z_all, bc_all, dt_all, wbuf, a_s, step_s, at_s, stept_s,
     stl, msg, st_in, inc_s, e_s, y_s, g_s, adx, ad_in, ag_own, ag_all, gb_own, gb_in, comb, comb_c, comb2, comb_f,
@@ -74,7 +74,7 @@
     h1 = copy(x_ref.at[L - 16 : L, :], halo_x, h_ss.at[0], h_rs.at[0], place(nxt))
     h2 = copy(bc_ref.at[L - 16 : L, :], halo_bc, h_ss.at[1], h_rs.at[1], place(nxt))
     own_rows = pl.ds(pl.multiple_of(t * L, L), L)
-    dts = [copy(dt_ref, dt_all.at[own_rows, :], dt_ss.at[e], dt_rs.at[e], {"tensor": tp(e)}) for e in range(1, nt)]
+    dts = [copy(dt_ref, dt_all.at[t], dt_ss.at[e], dt_rs.at[e], {"tensor": tp(e)}) for e in range(1, nt)]
     share = pl.ds(pl.multiple_of(c * R, 16), R)
     ws = [
         copy(w_ref.at[share, :], wbuf.at[d, share, :], w_ss.at[d], w_rs.at[d], {"fsdp": lax.rem(f + d, nf)})
@@ -85,8 +85,13 @@
     own_cols = pl.ds(pl.multiple_of(t * LW, 128), LW)
     own_z = pltpu.make_async_copy(z_ref.at[:, own_cols], z_all.at[own_rows, :], loc.at[1])
     own_z.start()
-    dt_all[own_rows, :] = dt_ref[...]
-
+    dt_all[t] = dt_ref[...]
+
+    def send_gate(e):
+        cols = pl.ds(pl.multiple_of(tp(e) * LW, 128), LW)
+        return copy(z_ref.at[:, cols], z_all.at[own_rows, :], z_ss.at[e], z_rs.at[e], {"tensor": tp(e)})
+
+    zs = [send_gate(1)]
     h1.wait()
     h2.wait()
     live = (idx > 0).astype(F32)
@@ -107,7 +112,7 @@
         copy(bc_all.at[own_rows, :], bc_all.at[own_rows, :], bc_ss.at[e], bc_rs.at[e], {"tensor": tp(e)})
         for e in range(1, nt)
     ]
-    xs, zs = [], []
+    xs = []
 
     def conv_group(e, store):
         base = tp(e) * LW
@@ -125,9 +130,8 @@
 
         conv_group(e, put)
         xs.append(copy(x_send.at[e - 1], x_all.at[own_rows, :], x_ss.at[e], x_rs.at[e], {"tensor": tp(e)}))
-    for e in range(1, nt):
-        cols = pl.ds(pl.multiple_of(tp(e) * LW, 128), LW)
-        zs.append(copy(z_ref.at[:, cols], z_all.at[own_rows, :], z_ss.at[e], z_rs.at[e], {"tensor": tp(e)}))
+    for e in range(2, nt):
+        zs.append(send_gate(e))
 
     def put_own(lanes, val):
         x_all[own_rows, lanes] = val
@@ -142,11 +146,15 @@
     for cp in dts:
         cp.wait()
     HR = at_s.shape[1]
-    sel = ((iota((128, 128), 0) == iota((128, 128), 1) + t * hl) & (iota((128, 128), 1) < hl)).astype(BF)
-    sel_t = ((iota((HR, 128), 1) == iota((HR, 128), 0) + t * hl) & (iota((HR, 128), 0) < hl)).astype(BF)
+    HA = dt_ref.shape[0]
+    sel = ((iota((HA, 128), 0) == iota((HA, 128), 1) + t * hl) & (iota((HA, 128), 1) < hl)).astype(BF)
+    sel_t = ((iota((HR, HA), 1) == iota((HR, HA), 0) + t * hl) & (iota((HR, HA), 0) < hl)).astype(BF)
     eye = (iota((HR, 128), 0) == iota((HR, 128), 1)).astype(F32)
-    hp = hp_ref[...]
-    hp_t = dot(eye, hp, 1, 1, HI)
+    place_head = (iota((hl, 128), 0) == iota((hl, 128), 1)).astype(F32)
+    hp = [
+        dot(jnp.broadcast_to(v[...], (8, hl)), place_head, precision=HI)[0:1, :] for v in (sb_ref, dr_ref, sk_ref)
+    ]
+    hp_t = [dot(eye, jnp.broadcast_to(v, (8, 128)), 1, 1, HI)[:, 0:1] for v in hp[0:2]]
     tri = (iota((L, L), 0) >= iota((L, L), 1)).astype(F32)
 
     def softplus(v):
@@ -154,13 +162,13 @@
 
     for b in range(nt):
         rows = slice(b * L, (b + 1) * L)
-        raw = dt_all[rows, :]
-        step = softplus(dot(raw, sel) + hp[0:1, :])
+        raw = dt_all[b]
+        step = softplus(dot(raw, sel, 0, 0) + hp[0])
         step_s[rows, :] = step
-        a_s[rows, :] = dot(tri, -step * jnp.exp(hp[1:2, :]), precision=HI)
-        step_t = softplus(dot(sel_t, raw, 1, 1) + hp_t[:, 0:1])
+        a_s[rows, :] = dot(tri, -step * jnp.exp(hp[1]), precision=HI)
+        step_t = softplus(dot(sel_t, raw) + hp_t[0])
         stept_s[b] = step_t
-        at_s[b] = dot(-step_t * jnp.exp(hp_t[:, 1:2]), tri, 1, 1, HI)
+        at_s[b] = dot(-step_t * jnp.exp(hp_t[1]), tri, 1, 1, HI)
     for cp in bcs:
         cp.wait()
     for cp in xs:
@@ -219,7 +227,7 @@
     for cp in zs:
         cp.wait()
     own_z.wait()
-    skip = spread(hp[2:3, :])[0:1, :]
+    skip = spread(hp[2])[0:1, :]
     ones = jnp.ones((8, LW), BF)
 
     def gate(b, carry):
@@ -282,18 +290,6 @@
         for e in range(1, nt)
     ]
     sent += scatter(0)
-    wfs = []
-    for d in range(1, nf):
-        ws[d - 1].wait()
-        wfs.append([
-            copy(wbuf.at[d, share, :], wbuf.at[d, share, :], wf_ss.at[d, k], wf_rs.at[d, k], {"context": lax.rem(c + k, nc)})
-            for k in range(1, nc)
-        ])
-    for d in range(1, 2):
-        for cp in wfs[d - 1]:
-            cp.wait()
-        project(d)
-        sent += scatter(d)
     for cp in ags + gbs:
         cp.wait()
     ag_all[t] = ag_own[...]
@@ -306,19 +302,25 @@
         acc = acc + gb_in[e]
     comb[:, LW : LW + part] = acc
     ccs = [copy(comb, comb_c.at[k], cc_ss.at[k], cc_rs.at[k], {"context": lax.rem(c + k, nc)}) for k in range(1, nc)]
-    for d in range(2, nf):
+    wfs = []
+    for d in range(1, nf):
+        ws[d - 1].wait()
+        wfs.append([
+            copy(wbuf.at[d, share, :], wbuf.at[d, share, :], wf_ss.at[d, k], wf_rs.at[d, k], {"context": lax.rem(c + k, nc)})
+            for k in range(1, nc)
+        ])
+    for cp in ccs:
+        cp.wait()
+    acc = comb[...]
+    for k in range(1, nc):
+        acc = acc + comb_c[k]
+    comb2[...] = acc
+    cfs = [copy(comb2, comb_f.at[k], cf_ss.at[k], cf_rs.at[k], {"fsdp": lax.rem(f + k, nf)}) for k in range(1, nf)]
+    for d in range(1, nf):
         for cp in wfs[d - 1]:
             cp.wait()
         project(d)
         sent += scatter(d)
-        if d == 2:
-            for cp in ccs:
-                cp.wait()
-            acc = comb[...]
-            for k in range(1, nc):
-                acc = acc + comb_c[k]
-            comb2[...] = acc
-            cfs = [copy(comb2, comb_f.at[k], cf_ss.at[k], cf_rs.at[k], {"fsdp": lax.rem(f + k, nf)}) for k in range(1, nf)]
     for cp in cfs:
         cp.wait()
     acc = comb2[...]
@@ -352,15 +354,14 @@
     HR = -(-hl // 8) * 8
     T = nt * L
     part = M // nt
-    hp = jnp.pad(jnp.stack([step_bias, rate, skip]), ((0, 5), (0, 128 - hl)))
-    dt = jnp.pad(dt[0], ((0, 0), (0, 128 - dt.shape[2])))
+    dt = dt[0].T
     vm = pl.BlockSpec(memory_space=pltpu.VMEM)
     hbm = pl.BlockSpec(memory_space=pl.ANY)
     V = pltpu.VMEM
     D = pltpu.SemaphoreType.DMA
     scratch = [
         V((16, full), BF), V((16, BC), BF), V((nt - 1, L, LW), BF), V((T, LW), BF), V((T, LW), BF),
-        V((T, BC), BF), V((T, 128), BF), V((nf, LW, W), BF), V((T, 128), F32), V((T, 128), F32),
+        V((T, BC), BF), V((nt,) + dt.shape, BF), V((nf, LW, W), BF), V((T, 128), F32), V((T, 128), F32),
         V((nt, HR, L), F32), V((nt, HR, L), F32),
         V((nt, N + 8, LW), F32), V((N + 8, LW), F32), V((nc, N + 8, LW), F32), V((N, LW), F32),
         V((128, LW), F32), V((T, LW), F32), V((T, LW), BF), V((nt, 24, L), F32), V((nt, 24, L), F32),
@@ -379,13 +380,13 @@
             jax.ShapeDtypeStruct((16, LW), F32),
             jax.ShapeDtypeStruct((16, M), F32),
         ),
-        in_specs=[vm, vm, hbm, vm, vm, vm, vm, vm, hbm, vm, vm, vm],
+        in_specs=[vm, vm, hbm, vm, vm, vm, vm, vm, vm, vm, hbm, vm, vm, vm],
         out_specs=(vm, vm, vm),
         scratch_shapes=scratch,
         compiler_params=pltpu.CompilerParams(
             collective_id=0, has_side_effects=True, vmem_limit_bytes=62 * 1024 * 1024
         ),
-    )(x[0], bc[0], z[0], dt, taps, bias[None], hp, gain[None], w, down.T, up, cot[0])
+    )(x[0], bc[0], z[0], dt, taps, bias[None], step_bias[None], rate[None], skip[None], gain[None], w, down.T, up, cot[0])
     return mixed[None], ga.T, gb
 
 

time: 119 us -> 116 us (0.975)
  local copies, waits for them, and re-layouts: 7.43 us -> 5.97 us
  other arithmetic: 1.29 us -> 0 us
    another operation x1 -> x0, other arithmetic: 1.29 us -> none  [shards(): hp = jnp.pad(jnp.stack([step_bias, rate, skip]), ((0, 5), (0, 128 - hl)))]
    unnamed x8 -> x7, local copies, waits for them, and re-layouts: 4.15 us -> 3.32 us
where the time goes in v2:
time: 116 us
  Pallas kernels  109 us (94%)
  local copies, waits for them, and re-layouts  5.97 us (5%)
    pallas_call x1, Pallas kernels, shards(): pl.pallas_call(functools.partial(kernel, nt, nf, nc, hl), out_shape=(jax....  109 us
    unnamed x7, local copies, waits for them, and re-layouts  3.32 us

profile of v2, /device:TPU:24, one launch (start us, length us, event | category | flops | bytes accessed | tf_op | source)
XLA Modules:
  0.0 115.7 jit_solution(4425383433896568508)
XLA Ops:
  0.6 1.3 %broadcast_in_dim.22.gain_ref = f32[1,1280]{1,0:T(1,128)} reshape(f32[1280]{0:T(1024)} %param.23) | data formatting | bytes 10240 | tf_op jit(solution)/shard_map/broadcast_in_dim | solution.py:389
  1.9 1.4 %broadcast_in_dim.18.bias_ref = f32[1,5376]{1,0:T(1,128)} reshape(f32[5376]{0:T(1024)} %param.19) | data formatting | bytes 43008 | tf_op jit(solution)/shard_map/broadcast_in_dim | solution.py:389
  3.3 109.1 %shard_map.157 = (bf16[128,2560]{1,0:T(8,128)(2,1)}, f32[16,1280]{1,0:T(8,128)}, f32[16,2560]{1,0:T(8,128)}) custom-call(bf16[128,5120]{1,0:T(8,128)(2,1)} %bitcast.13, bf16[128,256]{1,0:T(8,128)(2,1)} %bitcast.18, bf16[128,5120]{1,0:T(8,128)(2,1)} %bitcast.14, bf16[80,128]{1,0:T(8,128)(2,1)} %bitcast.20, f32[4,5376]{1,0:T(4,128)} %taps_ref.1, ...), custom_call_target="tpu_custom_call" | custom-call | tf_op jit(solution)/shard_map/pallas_call | solution.py:376
  112.4 0.0 copy-start.1
  112.4 0.0 copy-start
  112.4 2.0 %copy.20 = bf16[1,128,2560]{2,1,0:T(8,128)(2,1)} copy(bf16[1,128,2560]{2,1,0:T(8,128)(2,1)} %bitcast.15) | data formatting | bytes 1310720
  114.4 0.0 copy-done.1
  114.4 0.6 copy.21
  115.0 0.0 copy-done
  115.0 0.7 copy.22
Async XLA Ops:
  112.4 2.0 %copy-start.1 = (f32[16,1280]{1,0:T(8,128)S(1)}, f32[16,1280]{1,0:T(8,128)}, u32[]{:S(2)}) copy-start(f32[16,1280]{1,0:T(8,128)} %get-tuple-element.7) | copy-start | bytes 245764
  112.4 2.7 %copy-start = (f32[16,2560]{1,0:T(8,128)S(1)}, f32[16,2560]{1,0:T(8,128)}, u32[]{:S(2)}) copy-start(f32[16,2560]{1,0:T(8,128)} %get-tuple-element.14) | copy-start | bytes 491524
